TPU v7x, 128 devices: a whole 4x4x4 slice. The times are simulated.
128 devices in a mesh: dp: 16 (over x_lo, z, core), expert: 8 (over y, x_hi).
Axes of the slice: x: 4 (x_hi: 2, x_lo: 2; x = x_hi * 2 + x_lo), y: 4, z: 4, core: 2. Of those that a mesh axis runs over, the one named last changes fastest.
Arguments:
- tokens: bfloat16 [16384, 2048], P(('dp', 'expert')), may hold values from -6 to 6
- norm_gain: float32 [2048], replicated, may hold values from 0.25 to 1.75
- router_weight: bfloat16 [2048, 64], P('dp'), may hold values from -0.25 to 0.25
- expert_ids: int32 [16384, 8], P(('dp', 'expert')), may hold values from 0 to 63, all different within a row; in each aligned block of 128 rows (0 to 127, 128 to 255, ...) at most 32 rows name the same one
- gate_weight: bfloat16 [8, 2048, 1024], P('expert', 'dp'), may hold values from -0.125 to 0.125
- up_weight: bfloat16 [8, 2048, 1024], P('expert', 'dp'), may hold values from -0.125 to 0.125
- down_weight: bfloat16 [8, 2048, 1024], P('expert', 'dp'), may hold values from -0.1875 to 0.1875
- cotangent: bfloat16 [16384, 2048], P(('dp', 'expert')), may hold values from -6 to 6
Outputs:
- mixed: bfloat16 [16384, 2048], P(('dp', 'expert'))
- d_tokens: bfloat16 [16384, 2048], P(('dp', 'expert'))
- d_gain: float32 [2048], replicated
- d_router: float32 [2048, 64], P('dp')
- d_gate: bfloat16 [8, 2048, 1024], P('expert', 'dp')
- d_up: bfloat16 [8, 2048, 1024], P('expert', 'dp')
- d_down: bfloat16 [8, 2048, 1024], P('expert', 'dp')
Inputs may be any that keep to these rules, and one draw needn't show every extreme that they name: `expert_ids`: each row names 8 different experts; in the rows of one device no expert is named more than 32 times.
All inputs are finite; a program needn't handle non-finite values.
Results may differ from a plain program's by a relative error of at most 0.018.
Values may be sent and summed in bfloat16 or wider, within the bound.
No kernel may reach another device: no remote copies, remote signals or barrier semaphores. Data moves between devices by JAX's collectives and lax.ppermute only.
A program may use at most 128 MiB of HBM per device.

v0:
```python
import jax
import jax.numpy as jnp
from jax import lax
from jax.sharding import PartitionSpec as P

D = 2048
FF = 1024
CAP = 32
EPSILON = 1e-05
HIGHEST = lax.Precision.HIGHEST


def in_one_piece(arrays, axis, dim, along):
    both = jnp.concatenate(arrays, axis=along)
    result, at, finished = (lax.all_gather(both, axis, axis=dim, tiled=True), 0, [])
    for a in arrays:
        finished.append(lax.slice_in_dim(result, at, at + a.shape[along], axis=along))
        at += a.shape[along]
    return tuple(finished)


def split_up(x, dim, length):
    shape = x.shape
    pieces = x.reshape(*shape[:dim], length, shape[dim] // length, *shape[dim + 1 :])
    return jnp.moveaxis(pieces, dim, 0)


def sum_at_owner(x, axis, dim):
    length = lax.axis_size(axis)
    pieces = lax.all_to_all(split_up(x, dim, length), axis, 0, 0, tiled=True)
    return jnp.sum(pieces.astype(jnp.float32), axis=0)


def copy_for_each(x, axis):
    copies = jnp.broadcast_to(x, (lax.axis_size(axis), *x.shape))
    return lax.all_to_all(copies, axis, split_axis=0, concat_axis=0, tiled=True)


def over_copies(x, axis):
    everything = copy_for_each(x, axis)
    return jnp.sum(everything.astype(jnp.float32), axis=0)


def normalize(inputs, norm_gain):
    meansq = jnp.mean(inputs * inputs, axis=-1, keepdims=True)
    return inputs * lax.rsqrt(meansq + EPSILON) * norm_gain


def gate_weights(logits, expert_ids):
    member = (
        expert_ids[:, :, None] == jnp.arange(logits.shape[-1], dtype=jnp.int32)[None, None, :]
    ).astype(jnp.float32)
    picked = jnp.sum(member * logits[:, None, :], axis=-1)
    raised = jnp.exp(picked)
    return raised / jnp.sum(raised, axis=-1, keepdims=True)


def pick_matrix(expert_ids, window, capacity):
    flat_ids = expert_ids.reshape(-1)
    chosen = (flat_ids[:, None] == jnp.arange(window, dtype=jnp.int32)[None, :]).astype(jnp.int32)
    before = jnp.cumsum(chosen, axis=0, dtype=jnp.int32) - chosen
    position = jnp.sum(before * chosen, axis=-1)
    target = jnp.where(flat_ids < window, flat_ids * capacity + position, -1)
    columns = jnp.arange(window * capacity, dtype=jnp.int32)
    matrix = (target[:, None] == columns[None, :]).astype(jnp.float32)
    return matrix.reshape(expert_ids.shape[0], expert_ids.shape[1], window * capacity)


def expert_forward(slot_rows, w_gate, w_up, w_down):
    gate_pre = jnp.dot(slot_rows, w_gate, preferred_element_type=jnp.float32)
    up_pre = jnp.dot(slot_rows, w_up, preferred_element_type=jnp.float32)
    active = (gate_pre * jax.nn.sigmoid(gate_pre) * up_pre).astype(jnp.bfloat16)
    output = jnp.dot(active, w_down.T, preferred_element_type=jnp.float32).astype(jnp.bfloat16)
    return (output, gate_pre, up_pre)


def expert_backward(slot_grads, gate_pre, up_pre, w_gate, w_up, w_down):
    sigmoid_gate = jax.nn.sigmoid(gate_pre)
    active = (gate_pre * sigmoid_gate * up_pre).astype(jnp.bfloat16)
    back = jnp.dot(slot_grads, w_down, preferred_element_type=jnp.float32)
    grad_gate = (back * up_pre * sigmoid_gate * (1.0 + gate_pre * (1.0 - sigmoid_gate))).astype(
        jnp.bfloat16
    )
    grad_upper = (back * gate_pre * sigmoid_gate).astype(jnp.bfloat16)
    grad_rows = jnp.dot(grad_gate, w_gate.T, preferred_element_type=jnp.float32)
    grad_rows = (
        grad_rows + jnp.dot(grad_upper, w_up.T, preferred_element_type=jnp.float32)
    ).astype(jnp.bfloat16)
    return (grad_rows, active, grad_gate, grad_upper)


def body(
    tokens, norm_gain, router_weight, expert_ids, gate_weight, up_weight, down_weight, cotangent
):
    window = lax.axis_size("expert")
    slot_count = window * CAP
    router_full = lax.all_gather(router_weight, "dp", axis=0, tiled=True)
    inputs = tokens.astype(jnp.float32)
    hidden = normalize(inputs, norm_gain).astype(jnp.bfloat16)
    logits = jnp.dot(hidden, router_full, preferred_element_type=jnp.float32)
    weights, gate_back = jax.vjp(lambda values: gate_weights(values, expert_ids), logits)
    pick_table = pick_matrix(expert_ids, window, CAP)
    spread_half = jnp.sum(pick_table, axis=1).astype(jnp.bfloat16)
    blending = jnp.einsum("tks,tk->ts", pick_table, weights, precision=HIGHEST)
    outgoing = (
        jnp.dot(spread_half.T, hidden, preferred_element_type=jnp.float32)
        .astype(jnp.bfloat16)
        .reshape(window, CAP, D)
    )
    weights_full = in_one_piece((gate_weight, up_weight, down_weight), "dp", 1, 0)
    w_gate = weights_full[0][0]
    w_up = weights_full[1][0]
    w_down = weights_full[2][0]
    arrived_rows = lax.all_to_all(outgoing, "expert", split_axis=0, concat_axis=0, tiled=True)
    lead = arrived_rows.shape[0]
    middle = arrived_rows.shape[1]
    output, gate_pre, up_pre = expert_forward(arrived_rows.reshape(-1, D), w_gate, w_up, w_down)
    produced = output.reshape(lead, middle, D)
    gate_slots = gate_pre.reshape(lead, middle, FF)
    upper_slots = up_pre.reshape(lead, middle, FF)
    returned = lax.all_to_all(produced, "expert", split_axis=0, concat_axis=0, tiled=True).reshape(
        slot_count, D
    )
    returned_wide = returned.astype(jnp.float32)
    mixed_out = jnp.dot(blending, returned_wide, precision=HIGHEST).astype(jnp.bfloat16)
    gathered_cot = jnp.dot(spread_half.T, cotangent, preferred_element_type=jnp.float32)
    per_slot = jnp.sum(gathered_cot * returned_wide, axis=-1)
    grad_weights = jnp.einsum("tks,s->tk", pick_table, per_slot, precision=HIGHEST)
    grad_logits = gate_back(grad_weights)[0]
    outgoing_grad = (
        jnp.dot(blending.T, cotangent.astype(jnp.float32), precision=HIGHEST)
        .astype(jnp.bfloat16)
        .reshape(window, CAP, D)
    )
    arrived_grad = lax.all_to_all(outgoing_grad, "expert", split_axis=0, concat_axis=0, tiled=True)
    flat_rows = arrived_rows.reshape(-1, D)
    flat_grads = arrived_grad.reshape(-1, D)
    grad_rows, active, grad_gate, grad_upper = expert_backward(
        flat_grads, gate_slots.reshape(-1, FF), upper_slots.reshape(-1, FF), w_gate, w_up, w_down
    )
    grad_back = lax.all_to_all(
        grad_rows.reshape(window, CAP, D), "expert", split_axis=0, concat_axis=0, tiled=True
    ).reshape(slot_count, D)
    term_gate = jnp.dot(flat_rows.T, grad_gate, preferred_element_type=jnp.float32)
    term_upper = jnp.dot(flat_rows.T, grad_upper, preferred_element_type=jnp.float32)
    term_down = jnp.dot(flat_grads.T, active, preferred_element_type=jnp.float32)
    summed = lax.psum_scatter(
        jnp.concatenate([term_gate, term_upper, term_down], axis=1).astype(jnp.bfloat16),
        "dp",
        scatter_dimension=0,
        tiled=True,
    ).astype(jnp.float32)
    grad_hidden = jnp.dot(spread_half, grad_back, preferred_element_type=jnp.float32)
    grad_hidden = grad_hidden + jnp.dot(
        grad_logits, router_full.astype(jnp.float32).T, precision=HIGHEST
    )
    unused_value, norm_back = jax.vjp(normalize, inputs, norm_gain)
    grad_inputs, grad_gain = norm_back(grad_hidden)
    grad_router = jnp.dot(hidden.astype(jnp.float32).T, grad_logits, precision=HIGHEST)
    router_part = sum_at_owner(grad_router.astype(jnp.bfloat16), "dp", 0)
    router_mine = over_copies(router_part.astype(jnp.bfloat16), "expert").astype(jnp.float32)
    gain_sum = lax.psum(grad_gain, ("dp", "expert"))
    grad_gate_out = summed[:, :FF].astype(jnp.bfloat16)[None]
    grad_up_out = summed[:, FF : 2 * FF].astype(jnp.bfloat16)[None]
    grad_down_out = summed[:, 2 * FF :].astype(jnp.bfloat16)[None]
    return (
        mixed_out,
        grad_inputs.astype(jnp.bfloat16),
        gain_sum,
        router_mine,
        grad_gate_out,
        grad_up_out,
        grad_down_out,
    )


def solution(mesh):
    in_specs = (
        P(("dp", "expert"), None),
        P(),
        P("dp", None),
        P(("dp", "expert"), None),
        P("expert", "dp", None),
        P("expert", "dp", None),
        P("expert", "dp", None),
        P(("dp", "expert"), None),
    )
    out_specs = (
        P(("dp", "expert"), None),
        P(("dp", "expert"), None),
        P(),
        P("dp", None),
        P("expert", "dp", None),
        P("expert", "dp", None),
        P("expert", "dp", None),
    )
    return jax.shard_map(body, mesh=mesh, in_specs=in_specs, out_specs=out_specs, check_vma=False)
```

profile of v0, /device:TPU:1, one launch (start us, length us, event | category | flops | bytes accessed | tf_op | source)
XLA Modules:
  0.0 330.0 jit_solution(3319858266487233548)
XLA Ops:
  7.3 2.2 pad_maximum_fusion.1
  9.5 0.8 copy.56
  10.2 0.1 eq.57
  10.3 0.1 eq.53
  10.4 2.3 reduce-window.6
  12.7 0.3 slice_reduce_fusion
  13.0 0.2 reduce-window.9
  13.2 0.1 add_bitcast_fusion
  13.3 0.1 reduce_sum.114
  13.4 0.7 add_select_fusion
  14.1 0.1 copy.59
  14.2 0.4 convert_reduce_fusion
  14.6 1.2 fusion.16
  15.9 2.5 convolution_convert_fusion.3
  18.4 7.5 %all-to-all-start = ((bf16[8,32,2048]{2,1,0:T(8,128)(2,1)}), bf16[8,32,2048]{2,1,0:T(8,128)(2,1)S(1)}, u32[]{:S(2)}, u32[]{:S(2)}) async-start(bf16[8,32,2048]{2,1,0:T(8,128)(2,1)} %bitcast.3), calls=%async_computation | async-start | bytes 2097152 | tf_op jit(solution)/shard_map/all_to_all | solution.py:114
  25.9 41.0 %all_gather.6 = bf16[2048,64]{0,1:T(8,128)(2,1)S(1)} all-gather(bf16[128,64]{0,1:T(8,128)(2,1)S(1)} %copy-done.14), channel_id=1, replica_groups=mesh['dp'=16,'expert'=8] {'dp'}, dimensions={0}, use_global_device_ids=true | all-gather | bytes 278528 | tf_op jit(solution)/shard_map/all_gather | solution.py:97
  67.0 0.7 copy-done.2
  67.7 0.4 fusion.41
  68.1 0.1 copy.65
  68.2 0.7 fusion.19
  69.0 2.1 convolution_convert_fusion.4
  71.1 6.8 %all-to-all-start.2 = ((bf16[8,32,2048]{2,1,0:T(8,128)(2,1)}), bf16[8,32,2048]{2,1,0:T(8,128)(2,1)S(1)}, u32[]{:S(2)}, u32[]{:S(2)}) async-start(bf16[8,32,2048]{2,1,0:T(8,128)(2,1)} %bitcast.109), calls=%async_computation.2 | async-start | bytes 2097152 | tf_op jit(solution)/shard_map/all_to_all | solution.py:135
  77.9 0.2 reduce-scatter.4.cloned.1.call-start
  78.1 30.4 %all-gather.2.cloned.1.call-done = bf16[3,2048,1024]{2,1,0:T(8,128)(2,1)} async-done(((bf16[3,128,1024]{2,1,0:T(8,128)(2,1)}), bf16[3,2048,1024]{2,1,0:T(8,128)(2,1)}) %all-gather.2.cloned.1.call-update) | async-done | bytes 12582928 | tf_op jit(solution)/shard_map/all_gather | solution.py:15
  108.5 4.4 %fusion.3 = f32[256,1024]{1,0:T(8,128)} fusion(bf16[256,2048]{1,0:T(8,128)(2,1)S(1)} %bitcast.100, bf16[3,2048,1024]{2,1,0:T(8,128)(2,1)} %all-gather.2.cloned.1.call-done), kind=kOutput, calls=%fused_computation.10 | convolution fusion | flops 1073741824 | bytes 6291456 | tf_op jit(solution)/shard_map/dot_general | solution.py:71
  112.9 4.4 %fusion.1 = f32[256,1024]{1,0:T(8,128)} fusion(bf16[256,2048]{1,0:T(8,128)(2,1)S(1)} %bitcast.101, bf16[3,2048,1024]{2,1,0:T(8,128)(2,1)} %all-gather.2.cloned.1.call-done), kind=kOutput, calls=%fused_computation.8 | convolution fusion | flops 1073741824 | bytes 6291456 | tf_op jit(solution)/shard_map/dot_general | solution.py:70
  117.3 4.4 %multiply_convert_fusion = (bf16[256,1024]{1,0:T(8,128)(2,1)S(1)}, bf16[256,1024]{1,0:T(8,128)(2,1)S(1)}, bf16[256,1024]{1,0:T(8,128)(2,1)S(1)}) fusion(f32[256,1024]{1,0:T(8,128)} %fusion.1, f32[256,1024]{1,0:T(8,128)} %fusion.3, bf16[256,2048]{1,0:T(8,128)(2,1)S(1)} %bitcast.104, bf16[3,2048,1024]{2,1,0:T(8,128)(2,1)} %all-gather.2.cloned.1.call-done), kind=kOutput, calls=%fused_computation.36 | convolution fusion | flops 1077936128 | bytes 8912896 | tf_op jit(solution)/shard_map/dot_general | solution.py:80
  121.7 1.3 convolution_convert_fusion
  123.1 1.3 convolution_convert_fusion.1
  124.4 1.3 convolution_convert_fusion.2
  125.7 21.2 %pad_maximum_fusion = bf16[2048,3072]{0,1:T(8,128)(2,1)} fusion(bf16[2048,1024]{0,1:T(8,128)(2,1)S(1)} %convolution_convert_fusion, bf16[2048,1024]{0,1:T(8,128)(2,1)S(1)} %convolution_convert_fusion.1, bf16[2048,1024]{0,1:T(8,128)(2,1)S(1)} %convolution_convert_fusion.2), kind=kLoop, calls=%fused_computation | loop fusion | flops 37748736 | bytes 25165824 | tf_op jit(solution)/shard_map/concatenate | solution.py:148
  146.9 16.6 %copy.68 = bf16[2048,3072]{1,0:T(8,128)(2,1)} copy(bf16[2048,3072]{0,1:T(8,128)(2,1)} %pad_maximum_fusion) | data formatting | bytes 25165824
  163.6 1.0 copy-done.8
  164.6 4.6 %fusion.8 = bf16[256,2048]{1,0:T(8,128)(2,1)} fusion(bf16[256,1024]{1,0:T(8,128)(2,1)S(1)} %copy-done.8, bf16[3,2048,1024]{2,1,0:T(8,128)(2,1)} %all-gather.2.cloned.1.call-done), kind=kOutput, calls=%fused_computation.17 | convolution fusion | flops 1074266112 | bytes 5767168 | tf_op jit(solution)/shard_map/dot_general | solution.py:73
  169.2 6.1 %all-to-all-start.1 = ((bf16[8,32,2048]{2,1,0:T(8,128)(2,1)}), bf16[8,32,2048]{2,1,0:T(8,128)(2,1)S(1)}, u32[]{:S(2)}, u32[]{:S(2)}) async-start(bf16[8,32,2048]{2,1,0:T(8,128)(2,1)} %bitcast.8), calls=%async_computation.1 | async-start | bytes 2097152 | tf_op jit(solution)/shard_map/all_to_all | solution.py:121
  175.3 3.5 %fusion = f32[256,2048]{1,0:T(8,128)S(1)} fusion(bf16[256,1024]{1,0:T(8,128)(2,1)S(1)} %copy-done.6, bf16[3,2048,1024]{2,1,0:T(8,128)(2,1)} %all-gather.2.cloned.1.call-done), kind=kOutput, calls=%fused_computation.7 | convolution fusion | flops 1073741824 | bytes 6815744 | tf_op jit(solution)/shard_map/dot_general | solution.py:85
  178.9 4.5 %fusion.7 = bf16[256,2048]{1,0:T(8,128)(2,1)} fusion(f32[256,2048]{1,0:T(8,128)S(1)} %fusion, bf16[256,1024]{1,0:T(8,128)(2,1)S(1)} %copy-done.4, bf16[3,2048,1024]{2,1,0:T(8,128)(2,1)} %all-gather.2.cloned.1.call-done), kind=kOutput, calls=%fused_computation.16 | convolution fusion | flops 1074790400 | bytes 7864320 | tf_op jit(solution)/shard_map/dot_general | solution.py:87
  183.4 14.9 %all-to-all-done.1 = bf16[8,32,2048]{2,1,0:T(8,128)(2,1)S(1)} async-done(((bf16[8,32,2048]{2,1,0:T(8,128)(2,1)}), bf16[8,32,2048]{2,1,0:T(8,128)(2,1)S(1)}, u32[]{:S(2)}, u32[]{:S(2)}) %all-to-all-start.1) | async-done | bytes 1048608 | tf_op jit(solution)/shard_map/all_to_all | solution.py:121
  198.3 3.6 %all-to-all-start.3 = ((bf16[8,32,2048]{2,1,0:T(8,128)(2,1)}), bf16[8,32,2048]{2,1,0:T(8,128)(2,1)S(1)}, u32[]{:S(2)}, u32[]{:S(2)}) async-start(bf16[8,32,2048]{2,1,0:T(8,128)(2,1)} %bitcast.110), calls=%async_computation.3 | async-start | bytes 2097152 | tf_op jit(solution)/shard_map/all_to_all | solution.py:141
  201.8 0.5 fusion.9
  202.4 3.6 %fusion.18 = f32[1,128,8]{2,0,1:T(1,128)S(1)} fusion(f32[256,1,1]{0,1,2:T(1,128)S(1)} %bitcast.115, s32[128,8]{1,0:T(8,128)S(1)} %copy.59), kind=kOutput, calls=%fused_computation.42 | convolution fusion | flops 3407872 | bytes 9216 | tf_op jit(solution)/shard_map/tks,s->tk/dot_general | solution.py:128
  206.0 0.1 copy.67
  206.2 0.5 fusion.12
  206.7 0.1 copy-done.11
  206.8 0.8 copy.86
  207.6 16.8 %all-to-all-done.3 = bf16[8,32,2048]{2,1,0:T(8,128)(2,1)S(1)} async-done(((bf16[8,32,2048]{2,1,0:T(8,128)(2,1)}), bf16[8,32,2048]{2,1,0:T(8,128)(2,1)S(1)}, u32[]{:S(2)}, u32[]{:S(2)}) %all-to-all-start.3) | async-done | bytes 1048608 | tf_op jit(solution)/shard_map/all_to_all | solution.py:141
  224.4 6.8 %all-to-all-start.4 = ((bf16[16,128,64]{1,2,0:T(8,128)(2,1)}), bf16[16,128,64]{1,2,0:T(8,128)(2,1)S(1)}, u32[]{:S(2)}, u32[]{:S(2)}) async-start(bf16[16,128,64]{1,2,0:T(8,128)(2,1)} %bitcast.98), calls=%async_computation.4 | async-start | bytes 524288 | tf_op jit(solution)/shard_map/all_to_all | solution.py:30
  231.2 0.3 fusion.44
  231.5 1.9 fusion.14
  233.4 0.6 multiply_multiply_fusion
  234.1 1.1 fusion.15
  235.2 5.1 %all-to-all-done.4 = bf16[16,128,64]{1,2,0:T(8,128)(2,1)S(1)} async-done(((bf16[16,128,64]{1,2,0:T(8,128)(2,1)}), bf16[16,128,64]{1,2,0:T(8,128)(2,1)S(1)}, u32[]{:S(2)}, u32[]{:S(2)}) %all-to-all-start.4) | async-done | bytes 262176 | tf_op jit(solution)/shard_map/all_to_all | solution.py:30
  240.3 0.7 broadcast_in_dim.44
  241.0 3.4 %all-to-all-start.5 = ((bf16[8,128,64]{1,2,0:T(8,128)(2,1)}), bf16[8,128,64]{1,2,0:T(8,128)(2,1)S(1)}, u32[]{:S(2)}, u32[]{:S(2)}) async-start(bf16[8,128,64]{1,2,0:T(8,128)(2,1)} %broadcast_in_dim.44), calls=%async_computation.5 | async-start | bytes 262144 | tf_op jit(solution)/shard_map/all_to_all | solution.py:36
  244.4 1.4 convolution_convert_fusion.5
  245.8 72.5 %psum.7 = f32[2048]{0:T(1024)} all-reduce(f32[2048]{0:T(1024)S(1)} %get-tuple-element.42), channel_id=1, replica_groups=mesh['dp'=16,'expert'=8] {'dp','expert'}, use_global_device_ids=true, to_apply=%region_12.13 | all-reduce | flops 2048 | bytes 16384 | tf_op jit(solution)/shard_map/psum | solution.py:162
  318.3 0.6 convert_reduce_fusion.1
  318.9 1.2 fusion.43
  320.1 0.2 copy.73
  320.3 0.9 copy.64
  321.1 0.2 copy.72
  321.3 0.9 copy.63
  322.1 0.2 copy.71
  322.3 0.9 copy.62
  (53 shorter events, 0.5 us)
Async XLA Ops:
  7.2 61.8 %copy-start = (bf16[128,2048]{1,0:T(8,128)(2,1)S(1)}, bf16[128,2048]{1,0:T(8,128)(2,1)}, u32[]{:S(2)}) copy-start(bf16[128,2048]{1,0:T(8,128)(2,1)} %param.15) | copy-start | bytes 1572868
  7.2 60.9 %copy-start.13 = (s32[128,8]{0,1:T(8,128)S(1)}, s32[128,8]{0,1:T(8,128)}, u32[]{:S(2)}) copy-start(s32[128,8]{0,1:T(8,128)} %param.11) | copy-start | bytes 12292
  7.2 60.5 %copy-start.1 = (bf16[128,2048]{1,0:T(8,128)(2,1)S(1)}, bf16[128,2048]{1,0:T(8,128)(2,1)}, u32[]{:S(2)}) copy-start(bf16[128,2048]{1,0:T(8,128)(2,1)} %param.8) | copy-start | bytes 1572868
  7.2 60.5 %copy-start.12 = (f32[2048]{0:T(1024)S(1)}, f32[2048]{0:T(1024)}, u32[]{:S(2)}) copy-start(f32[2048]{0:T(1024)} %param.9) | copy-start | bytes 24580
  7.2 18.7 %copy-start.14 = (bf16[128,64]{0,1:T(8,128)(2,1)S(1)}, bf16[128,64]{0,1:T(8,128)(2,1)}, u32[]{:S(2)}) copy-start(bf16[128,64]{0,1:T(8,128)(2,1)} %param.10) | copy-start | bytes 49156
  7.2 101.3 %all-gather.2.cloned.1.call-start = ((), (), s32[]{:S(2)}) async-start(), calls=%async_computation.7 | async-start | bytes 13369344 | tf_op jit(solution)/shard_map/all_gather | solution.py:15
  15.9 10.0 %copy-start.17 = (f32[128]{0:T(128)}, f32[128]{0:T(128)S(1)}, u32[]{:S(2)}) copy-start(f32[128]{0:T(128)S(1)} %fusion.16) | copy-start | bytes 1540
  15.9 190.3 %copy-start.15 = (f32[128]{0:T(128)}, f32[128]{0:T(128)S(1)}, u32[]{:S(2)}) copy-start(f32[128]{0:T(128)S(1)} %fusion.34) | copy-start | bytes 1540
  18.4 52.6 %all-to-all-start = ((bf16[8,32,2048]{2,1,0:T(8,128)(2,1)}), bf16[8,32,2048]{2,1,0:T(8,128)(2,1)S(1)}, u32[]{:S(2)}, u32[]{:S(2)}) async-start(bf16[8,32,2048]{2,1,0:T(8,128)(2,1)} %bitcast.3), calls=%async_computation | async-start | bytes 2097152 | tf_op jit(solution)/shard_map/all_to_all | solution.py:114
  67.0 0.7 copy-start.2
  69.0 2.1 copy-start.9
  71.1 46.3 %all-to-all-start.2 = ((bf16[8,32,2048]{2,1,0:T(8,128)(2,1)}), bf16[8,32,2048]{2,1,0:T(8,128)(2,1)S(1)}, u32[]{:S(2)}, u32[]{:S(2)}) async-start(bf16[8,32,2048]{2,1,0:T(8,128)(2,1)} %bitcast.109), calls=%async_computation.2 | async-start | bytes 2097152 | tf_op jit(solution)/shard_map/all_to_all | solution.py:135
  77.9 241.0 %reduce-scatter.4.cloned.1.call-start = ((), (), s32[]{:S(2)}) async-start(), calls=%async_computation.8 | async-start | bytes 13369344
  121.7 1.4 copy-start.7
  121.7 1.4 copy-start.3
  121.7 2.7 copy-start.5
  163.5 1.0 copy-start.8
  164.6 10.7 %copy-start.6 = (bf16[256,1024]{1,0:T(8,128)(2,1)S(1)}, bf16[256,1024]{1,0:T(8,128)(2,1)}, u32[]{:S(2)}) copy-start(bf16[256,1024]{1,0:T(8,128)(2,1)} %copy-done.5) | copy-start | bytes 1572868
  169.2 29.1 %all-to-all-start.1 = ((bf16[8,32,2048]{2,1,0:T(8,128)(2,1)}), bf16[8,32,2048]{2,1,0:T(8,128)(2,1)S(1)}, u32[]{:S(2)}, u32[]{:S(2)}) async-start(bf16[8,32,2048]{2,1,0:T(8,128)(2,1)} %bitcast.8), calls=%async_computation.1 | async-start | bytes 2097152 | tf_op jit(solution)/shard_map/all_to_all | solution.py:121
  175.3 3.5 %copy-start.4 = (bf16[256,1024]{1,0:T(8,128)(2,1)S(1)}, bf16[256,1024]{1,0:T(8,128)(2,1)}, u32[]{:S(2)}) copy-start(bf16[256,1024]{1,0:T(8,128)(2,1)} %copy-done.3) | copy-start | bytes 1572868
  198.3 26.1 %all-to-all-start.3 = ((bf16[8,32,2048]{2,1,0:T(8,128)(2,1)}), bf16[8,32,2048]{2,1,0:T(8,128)(2,1)S(1)}, u32[]{:S(2)}, u32[]{:S(2)}) async-start(bf16[8,32,2048]{2,1,0:T(8,128)(2,1)} %bitcast.110), calls=%async_computation.3 | async-start | bytes 2097152 | tf_op jit(solution)/shard_map/all_to_all | solution.py:141
  206.2 0.6 copy-start.11
  224.4 15.9 %all-to-all-start.4 = ((bf16[16,128,64]{1,2,0:T(8,128)(2,1)}), bf16[16,128,64]{1,2,0:T(8,128)(2,1)S(1)}, u32[]{:S(2)}, u32[]{:S(2)}) async-start(bf16[16,128,64]{1,2,0:T(8,128)(2,1)} %bitcast.98), calls=%async_computation.4 | async-start | bytes 524288 | tf_op jit(solution)/shard_map/all_to_all | solution.py:30
  231.2 2.9 copy-start.16
  231.5 12.9 %copy-start.10 = (f32[128,1,256]{2,1,0:T(1,128)S(1)}, f32[128,1,256]{2,1,0:T(1,128)}, u32[]{:S(2)}) copy-start(f32[128,1,256]{2,1,0:T(1,128)} %copy-done.9) | copy-start | bytes 393220
  241.0 77.3 %all-to-all-start.5 = ((bf16[8,128,64]{1,2,0:T(8,128)(2,1)}), bf16[8,128,64]{1,2,0:T(8,128)(2,1)S(1)}, u32[]{:S(2)}, u32[]{:S(2)}) async-start(bf16[8,128,64]{1,2,0:T(8,128)(2,1)} %broadcast_in_dim.44), calls=%async_computation.5 | async-start | bytes 262144 | tf_op jit(solution)/shard_map/all_to_all | solution.py:36
Sparse Core Ops, SparseCore 0:
  9.7 98.7 all-gather.1
  163.7 106.8 reduce-scatter.3
where the time goes:
time: 331 us; the launch traced here: 330 us
  blocking collectives  114 us (34%)
  waiting for transfers between devices  67.2 us (20%)
  matrix products  43.8 us (13%)
  starting transfers between devices  34.4 us (10%)
  other arithmetic  30.8 us (9%)
  local copies, waits for them, and re-layouts  25.9 us (8%)
  between operations  14.4 us (4%)
    psum x1, blocking collectives, body(): gain_sum = lax.psum(grad_gain, ('dp', 'expert'))  72.5 us
    all_gather x1, blocking collectives, body(): router_full = lax.all_gather(router_weight, 'dp', axis=0, tiled=True)  41 us
    all_gather x1, waiting for transfers between devices, in_one_piece(): lax.all_gather(both, axis, axis=dim, tiled=True)  30.4 us
    unnamed x44, local copies, waits for them, and re-layouts  22.4 us
    concatenate x1, other arithmetic, body(): jnp.concatenate([term_gate, term_upper, term_down], axis=1)  21.2 us
    all_to_all x1, waiting for transfers between devices, body(): lax.all_to_all(grad_rows.reshape(window, CAP, D), 'expert', split_axis=0,...  16.8 us
    all_to_all x1, waiting for transfers between devices, body(): lax.all_to_all(produced, 'expert', split_axis=0, concat_axis=0, tiled=True)  14.9 us
    all_to_all x1, starting transfers between devices, body(): lax.all_to_all(outgoing, 'expert', split_axis=0, concat_axis=0, tiled=True)  7.46 us
  transfers between devices with their start and end apart: 8, of which 4 were waited for; matrix products, arithmetic and copies ran while one was open for 14% of the time, Pallas kernels for 0%

commit v1 on v0

--- a/solution.py
+++ b/solution.py
@@ -159,7 +159,7 @@
     grad_router = jnp.dot(hidden.astype(jnp.float32).T, grad_logits, precision=HIGHEST)
     router_part = sum_at_owner(grad_router.astype(jnp.bfloat16), "dp", 0)
     router_mine = over_copies(router_part.astype(jnp.bfloat16), "expert").astype(jnp.float32)
-    gain_sum = lax.psum(grad_gain, ("dp", "expert"))
+    gain_sum = lax.psum(lax.psum(grad_gain, "dp"), "expert")
     grad_gate_out = summed[:, :FF].astype(jnp.bfloat16)[None]
     grad_up_out = summed[:, FF : 2 * FF].astype(jnp.bfloat16)[None]
     grad_down_out = summed[:, 2 * FF :].astype(jnp.bfloat16)[None]

time: 331 us -> 312 us (0.943); the launches traced: 330 us -> 307 us
  blocking collectives: 114 us -> 90.9 us
    psum x1 -> x2, blocking collectives: 72.5 us -> 49.8 us  [body(): gain_sum = lax.psum(lax.psum(grad_gain, 'dp'), 'expert')]
  transfers between devices with their start and end apart: 8 -> 8, of which waited for: 4 -> 4; matrix products, arithmetic and copies ran while one was open for 14% -> 15% of each run, Pallas kernels for 0% -> 0%
where the time goes in v1:
time: 312 us; the launch traced here: 307 us
  blocking collectives  90.9 us (29%)
  waiting for transfers between devices  67.2 us (22%)
  matrix products  43.8 us (14%)
  starting transfers between devices  34.4 us (11%)
  other arithmetic  30.8 us (10%)
  local copies, waits for them, and re-layouts  25.9 us (8%)
  between operations  14.4 us (5%)
    psum x2, blocking collectives, body(): gain_sum = lax.psum(lax.psum(grad_gain, 'dp'), 'expert')  49.8 us
    all_gather x1, blocking collectives, body(): router_full = lax.all_gather(router_weight, 'dp', axis=0, tiled=True)  41 us
    all_gather x1, waiting for transfers between devices, in_one_piece(): lax.all_gather(both, axis, axis=dim, tiled=True)  30.4 us
    unnamed x44, local copies, waits for them, and re-layouts  22.4 us
    concatenate x1, other arithmetic, body(): jnp.concatenate([term_gate, term_upper, term_down], axis=1)  21.2 us
    all_to_all x1, waiting for transfers between devices, body(): lax.all_to_all(grad_rows.reshape(window, CAP, D), 'expert', split_axis=0,...  16.8 us
    all_to_all x1, waiting for transfers between devices, body(): lax.all_to_all(produced, 'expert', split_axis=0, concat_axis=0, tiled=True)  14.9 us
    all_to_all x1, starting transfers between devices, body(): lax.all_to_all(outgoing, 'expert', split_axis=0, concat_axis=0, tiled=True)  7.46 us
  transfers between devices with their start and end apart: 8, of which 4 were waited for; matrix products, arithmetic and copies ran while one was open for 15% of the time, Pallas kernels for 0%

profile of v1, /device:TPU:1, one launch (start us, length us, event | category | flops | bytes accessed | tf_op | source)
XLA Modules:
  0.0 307.3 jit_solution(17884822598062070000)
XLA Ops:
  7.3 2.2 pad_maximum_fusion.1
  9.5 0.8 copy.56
  10.2 0.1 eq.57
  10.3 0.1 eq.53
  10.4 2.3 reduce-window.6
  12.7 0.3 slice_reduce_fusion
  13.0 0.2 reduce-window.9
  13.2 0.1 add_bitcast_fusion
  13.3 0.1 reduce_sum.114
  13.4 0.7 add_select_fusion
  14.1 0.1 copy.59
  14.2 0.4 convert_reduce_fusion
  14.6 1.2 fusion.16
  15.9 2.5 convolution_convert_fusion.3
  18.4 7.5 %all-to-all-start = ((bf16[8,32,2048]{2,1,0:T(8,128)(2,1)}), bf16[8,32,2048]{2,1,0:T(8,128)(2,1)S(1)}, u32[]{:S(2)}, u32[]{:S(2)}) async-start(bf16[8,32,2048]{2,1,0:T(8,128)(2,1)} %bitcast.3), calls=%async_computation | async-start | bytes 2097152 | tf_op jit(solution)/shard_map/all_to_all | solution.py:114
  25.9 41.0 %all_gather.6 = bf16[2048,64]{0,1:T(8,128)(2,1)S(1)} all-gather(bf16[128,64]{0,1:T(8,128)(2,1)S(1)} %copy-done.14), channel_id=1, replica_groups=mesh['dp'=16,'expert'=8] {'dp'}, dimensions={0}, use_global_device_ids=true | all-gather | bytes 278528 | tf_op jit(solution)/shard_map/all_gather | solution.py:97
  67.0 0.7 copy-done.2
  67.7 0.4 fusion.41
  68.1 0.1 copy.65
  68.2 0.7 fusion.19
  69.0 2.1 convolution_convert_fusion.4
  71.1 6.8 %all-to-all-start.2 = ((bf16[8,32,2048]{2,1,0:T(8,128)(2,1)}), bf16[8,32,2048]{2,1,0:T(8,128)(2,1)S(1)}, u32[]{:S(2)}, u32[]{:S(2)}) async-start(bf16[8,32,2048]{2,1,0:T(8,128)(2,1)} %bitcast.109), calls=%async_computation.2 | async-start | bytes 2097152 | tf_op jit(solution)/shard_map/all_to_all | solution.py:135
  77.9 0.2 reduce-scatter.4.cloned.1.call-start
  78.1 30.4 %all-gather.2.cloned.1.call-done = bf16[3,2048,1024]{2,1,0:T(8,128)(2,1)} async-done(((bf16[3,128,1024]{2,1,0:T(8,128)(2,1)}), bf16[3,2048,1024]{2,1,0:T(8,128)(2,1)}) %all-gather.2.cloned.1.call-update) | async-done | bytes 12582928 | tf_op jit(solution)/shard_map/all_gather | solution.py:15
  108.5 4.4 %fusion.3 = f32[256,1024]{1,0:T(8,128)} fusion(bf16[256,2048]{1,0:T(8,128)(2,1)S(1)} %bitcast.100, bf16[3,2048,1024]{2,1,0:T(8,128)(2,1)} %all-gather.2.cloned.1.call-done), kind=kOutput, calls=%fused_computation.10 | convolution fusion | flops 1073741824 | bytes 6291456 | tf_op jit(solution)/shard_map/dot_general | solution.py:71
  112.9 4.4 %fusion.1 = f32[256,1024]{1,0:T(8,128)} fusion(bf16[256,2048]{1,0:T(8,128)(2,1)S(1)} %bitcast.101, bf16[3,2048,1024]{2,1,0:T(8,128)(2,1)} %all-gather.2.cloned.1.call-done), kind=kOutput, calls=%fused_computation.8 | convolution fusion | flops 1073741824 | bytes 6291456 | tf_op jit(solution)/shard_map/dot_general | solution.py:70
  117.3 4.4 %multiply_convert_fusion = (bf16[256,1024]{1,0:T(8,128)(2,1)S(1)}, bf16[256,1024]{1,0:T(8,128)(2,1)S(1)}, bf16[256,1024]{1,0:T(8,128)(2,1)S(1)}) fusion(f32[256,1024]{1,0:T(8,128)} %fusion.1, f32[256,1024]{1,0:T(8,128)} %fusion.3, bf16[256,2048]{1,0:T(8,128)(2,1)S(1)} %bitcast.104, bf16[3,2048,1024]{2,1,0:T(8,128)(2,1)} %all-gather.2.cloned.1.call-done), kind=kOutput, calls=%fused_computation.36 | convolution fusion | flops 1077936128 | bytes 8912896 | tf_op jit(solution)/shard_map/dot_general | solution.py:80
  121.7 1.3 convolution_convert_fusion
  123.1 1.3 convolution_convert_fusion.1
  124.4 1.3 convolution_convert_fusion.2
  125.7 21.2 %pad_maximum_fusion = bf16[2048,3072]{0,1:T(8,128)(2,1)} fusion(bf16[2048,1024]{0,1:T(8,128)(2,1)S(1)} %convolution_convert_fusion, bf16[2048,1024]{0,1:T(8,128)(2,1)S(1)} %convolution_convert_fusion.1, bf16[2048,1024]{0,1:T(8,128)(2,1)S(1)} %convolution_convert_fusion.2), kind=kLoop, calls=%fused_computation | loop fusion | flops 37748736 | bytes 25165824 | tf_op jit(solution)/shard_map/concatenate | solution.py:148
  146.9 16.6 %copy.68 = bf16[2048,3072]{1,0:T(8,128)(2,1)} copy(bf16[2048,3072]{0,1:T(8,128)(2,1)} %pad_maximum_fusion) | data formatting | bytes 25165824
  163.6 1.0 copy-done.8
  164.6 4.6 %fusion.8 = bf16[256,2048]{1,0:T(8,128)(2,1)} fusion(bf16[256,1024]{1,0:T(8,128)(2,1)S(1)} %copy-done.8, bf16[3,2048,1024]{2,1,0:T(8,128)(2,1)} %all-gather.2.cloned.1.call-done), kind=kOutput, calls=%fused_computation.17 | convolution fusion | flops 1074266112 | bytes 5767168 | tf_op jit(solution)/shard_map/dot_general | solution.py:73
  169.2 6.1 %all-to-all-start.1 = ((bf16[8,32,2048]{2,1,0:T(8,128)(2,1)}), bf16[8,32,2048]{2,1,0:T(8,128)(2,1)S(1)}, u32[]{:S(2)}, u32[]{:S(2)}) async-start(bf16[8,32,2048]{2,1,0:T(8,128)(2,1)} %bitcast.8), calls=%async_computation.1 | async-start | bytes 2097152 | tf_op jit(solution)/shard_map/all_to_all | solution.py:121
  175.3 3.5 %fusion = f32[256,2048]{1,0:T(8,128)S(1)} fusion(bf16[256,1024]{1,0:T(8,128)(2,1)S(1)} %copy-done.6, bf16[3,2048,1024]{2,1,0:T(8,128)(2,1)} %all-gather.2.cloned.1.call-done), kind=kOutput, calls=%fused_computation.7 | convolution fusion | flops 1073741824 | bytes 6815744 | tf_op jit(solution)/shard_map/dot_general | solution.py:85
  178.9 4.5 %fusion.7 = bf16[256,2048]{1,0:T(8,128)(2,1)} fusion(f32[256,2048]{1,0:T(8,128)S(1)} %fusion, bf16[256,1024]{1,0:T(8,128)(2,1)S(1)} %copy-done.4, bf16[3,2048,1024]{2,1,0:T(8,128)(2,1)} %all-gather.2.cloned.1.call-done), kind=kOutput, calls=%fused_computation.16 | convolution fusion | flops 1074790400 | bytes 7864320 | tf_op jit(solution)/shard_map/dot_general | solution.py:87
  183.4 14.9 %all-to-all-done.1 = bf16[8,32,2048]{2,1,0:T(8,128)(2,1)S(1)} async-done(((bf16[8,32,2048]{2,1,0:T(8,128)(2,1)}), bf16[8,32,2048]{2,1,0:T(8,128)(2,1)S(1)}, u32[]{:S(2)}, u32[]{:S(2)}) %all-to-all-start.1) | async-done | bytes 1048608 | tf_op jit(solution)/shard_map/all_to_all | solution.py:121
  198.3 3.6 %all-to-all-start.3 = ((bf16[8,32,2048]{2,1,0:T(8,128)(2,1)}), bf16[8,32,2048]{2,1,0:T(8,128)(2,1)S(1)}, u32[]{:S(2)}, u32[]{:S(2)}) async-start(bf16[8,32,2048]{2,1,0:T(8,128)(2,1)} %bitcast.110), calls=%async_computation.3 | async-start | bytes 2097152 | tf_op jit(solution)/shard_map/all_to_all | solution.py:141
  201.8 0.5 fusion.9
  202.4 3.6 %fusion.18 = f32[1,128,8]{2,0,1:T(1,128)S(1)} fusion(f32[256,1,1]{0,1,2:T(1,128)S(1)} %bitcast.115, s32[128,8]{1,0:T(8,128)S(1)} %copy.59), kind=kOutput, calls=%fused_computation.42 | convolution fusion | flops 3407872 | bytes 9216 | tf_op jit(solution)/shard_map/tks,s->tk/dot_general | solution.py:128
  206.2 0.5 fusion.12
  206.7 0.1 copy-done.11
  206.8 0.8 copy.86
  207.6 16.8 %all-to-all-done.3 = bf16[8,32,2048]{2,1,0:T(8,128)(2,1)S(1)} async-done(((bf16[8,32,2048]{2,1,0:T(8,128)(2,1)}), bf16[8,32,2048]{2,1,0:T(8,128)(2,1)S(1)}, u32[]{:S(2)}, u32[]{:S(2)}) %all-to-all-start.3) | async-done | bytes 1048608 | tf_op jit(solution)/shard_map/all_to_all | solution.py:141
  224.4 6.8 %all-to-all-start.4 = ((bf16[16,128,64]{1,2,0:T(8,128)(2,1)}), bf16[16,128,64]{1,2,0:T(8,128)(2,1)S(1)}, u32[]{:S(2)}, u32[]{:S(2)}) async-start(bf16[16,128,64]{1,2,0:T(8,128)(2,1)} %bitcast.98), calls=%async_computation.4 | async-start | bytes 524288 | tf_op jit(solution)/shard_map/all_to_all | solution.py:30
  231.2 0.3 fusion.44
  231.5 1.9 fusion.14
  233.4 0.6 multiply_multiply_fusion
  234.1 1.1 fusion.15
  235.2 5.1 %all-to-all-done.4 = bf16[16,128,64]{1,2,0:T(8,128)(2,1)S(1)} async-done(((bf16[16,128,64]{1,2,0:T(8,128)(2,1)}), bf16[16,128,64]{1,2,0:T(8,128)(2,1)S(1)}, u32[]{:S(2)}, u32[]{:S(2)}) %all-to-all-start.4) | async-done | bytes 262176 | tf_op jit(solution)/shard_map/all_to_all | solution.py:30
  240.3 0.7 broadcast_in_dim.44
  241.0 3.4 %all-to-all-start.5 = ((bf16[8,128,64]{1,2,0:T(8,128)(2,1)}), bf16[8,128,64]{1,2,0:T(8,128)(2,1)S(1)}, u32[]{:S(2)}, u32[]{:S(2)}) async-start(bf16[8,128,64]{1,2,0:T(8,128)(2,1)} %broadcast_in_dim.44), calls=%async_computation.5 | async-start | bytes 262144 | tf_op jit(solution)/shard_map/all_to_all | solution.py:36
  244.4 1.4 convolution_convert_fusion.5
  245.8 28.3 %psum.14 = f32[2048]{0:T(1024)S(1)} all-reduce(f32[2048]{0:T(1024)S(1)} %get-tuple-element.42), channel_id=1, replica_groups=mesh['dp'=16,'expert'=8] {'dp'}, use_global_device_ids=true, to_apply=%region_12.13 | all-reduce | flops 2048 | bytes 16384 | tf_op jit(solution)/shard_map/psum | solution.py:162
  274.1 21.5 %psum.15 = f32[2048]{0:T(1024)} all-reduce(f32[2048]{0:T(1024)S(1)} %psum.14), channel_id=1, replica_groups=mesh['dp'=16,'expert'=8] {'expert'}, use_global_device_ids=true, to_apply=%region_13.14 | all-reduce | flops 2048 | bytes 16384 | tf_op jit(solution)/shard_map/psum | solution.py:162
  295.6 0.6 convert_reduce_fusion.1
  296.2 1.2 fusion.43
  297.4 0.2 copy.73
  297.6 0.9 copy.64
  298.4 0.2 copy.72
  298.6 0.9 copy.63
  299.4 0.2 copy.71
  299.6 0.9 copy.62
  (54 shorter events, 0.5 us)
Async XLA Ops:
  7.2 61.8 %copy-start = (bf16[128,2048]{1,0:T(8,128)(2,1)S(1)}, bf16[128,2048]{1,0:T(8,128)(2,1)}, u32[]{:S(2)}) copy-start(bf16[128,2048]{1,0:T(8,128)(2,1)} %param.15) | copy-start | bytes 1572868
  7.2 60.9 %copy-start.13 = (s32[128,8]{0,1:T(8,128)S(1)}, s32[128,8]{0,1:T(8,128)}, u32[]{:S(2)}) copy-start(s32[128,8]{0,1:T(8,128)} %param.11) | copy-start | bytes 12292
  7.2 60.5 %copy-start.1 = (bf16[128,2048]{1,0:T(8,128)(2,1)S(1)}, bf16[128,2048]{1,0:T(8,128)(2,1)}, u32[]{:S(2)}) copy-start(bf16[128,2048]{1,0:T(8,128)(2,1)} %param.8) | copy-start | bytes 1572868
  7.2 60.5 %copy-start.12 = (f32[2048]{0:T(1024)S(1)}, f32[2048]{0:T(1024)}, u32[]{:S(2)}) copy-start(f32[2048]{0:T(1024)} %param.9) | copy-start | bytes 24580
  7.2 18.7 %copy-start.14 = (bf16[128,64]{0,1:T(8,128)(2,1)S(1)}, bf16[128,64]{0,1:T(8,128)(2,1)}, u32[]{:S(2)}) copy-start(bf16[128,64]{0,1:T(8,128)(2,1)} %param.10) | copy-start | bytes 49156
  7.2 101.3 %all-gather.2.cloned.1.call-start = ((), (), s32[]{:S(2)}) async-start(), calls=%async_computation.7 | async-start | bytes 13369344 | tf_op jit(solution)/shard_map/all_gather | solution.py:15
  15.9 10.0 %copy-start.17 = (f32[128]{0:T(128)}, f32[128]{0:T(128)S(1)}, u32[]{:S(2)}) copy-start(f32[128]{0:T(128)S(1)} %fusion.16) | copy-start | bytes 1540
  15.9 190.3 %copy-start.15 = (f32[128]{0:T(128)}, f32[128]{0:T(128)S(1)}, u32[]{:S(2)}) copy-start(f32[128]{0:T(128)S(1)} %fusion.34) | copy-start | bytes 1540
  18.4 52.6 %all-to-all-start = ((bf16[8,32,2048]{2,1,0:T(8,128)(2,1)}), bf16[8,32,2048]{2,1,0:T(8,128)(2,1)S(1)}, u32[]{:S(2)}, u32[]{:S(2)}) async-start(bf16[8,32,2048]{2,1,0:T(8,128)(2,1)} %bitcast.3), calls=%async_computation | async-start | bytes 2097152 | tf_op jit(solution)/shard_map/all_to_all | solution.py:114
  67.0 0.7 copy-start.2
  69.0 2.1 copy-start.9
  71.1 46.3 %all-to-all-start.2 = ((bf16[8,32,2048]{2,1,0:T(8,128)(2,1)}), bf16[8,32,2048]{2,1,0:T(8,128)(2,1)S(1)}, u32[]{:S(2)}, u32[]{:S(2)}) async-start(bf16[8,32,2048]{2,1,0:T(8,128)(2,1)} %bitcast.109), calls=%async_computation.2 | async-start | bytes 2097152 | tf_op jit(solution)/shard_map/all_to_all | solution.py:135
  77.9 218.3 %reduce-scatter.4.cloned.1.call-start = ((), (), s32[]{:S(2)}) async-start(), calls=%async_computation.8 | async-start | bytes 13369344
  121.7 1.4 copy-start.7
  121.7 1.4 copy-start.3
  121.7 2.7 copy-start.5
  163.5 1.0 copy-start.8
  164.6 10.7 %copy-start.6 = (bf16[256,1024]{1,0:T(8,128)(2,1)S(1)}, bf16[256,1024]{1,0:T(8,128)(2,1)}, u32[]{:S(2)}) copy-start(bf16[256,1024]{1,0:T(8,128)(2,1)} %copy-done.5) | copy-start | bytes 1572868
  169.2 29.1 %all-to-all-start.1 = ((bf16[8,32,2048]{2,1,0:T(8,128)(2,1)}), bf16[8,32,2048]{2,1,0:T(8,128)(2,1)S(1)}, u32[]{:S(2)}, u32[]{:S(2)}) async-start(bf16[8,32,2048]{2,1,0:T(8,128)(2,1)} %bitcast.8), calls=%async_computation.1 | async-start | bytes 2097152 | tf_op jit(solution)/shard_map/all_to_all | solution.py:121
  175.3 3.5 %copy-start.4 = (bf16[256,1024]{1,0:T(8,128)(2,1)S(1)}, bf16[256,1024]{1,0:T(8,128)(2,1)}, u32[]{:S(2)}) copy-start(bf16[256,1024]{1,0:T(8,128)(2,1)} %copy-done.3) | copy-start | bytes 1572868
  198.3 26.1 %all-to-all-start.3 = ((bf16[8,32,2048]{2,1,0:T(8,128)(2,1)}), bf16[8,32,2048]{2,1,0:T(8,128)(2,1)S(1)}, u32[]{:S(2)}, u32[]{:S(2)}) async-start(bf16[8,32,2048]{2,1,0:T(8,128)(2,1)} %bitcast.110), calls=%async_computation.3 | async-start | bytes 2097152 | tf_op jit(solution)/shard_map/all_to_all | solution.py:141
  206.2 0.6 copy-start.11
  224.4 15.9 %all-to-all-start.4 = ((bf16[16,128,64]{1,2,0:T(8,128)(2,1)}), bf16[16,128,64]{1,2,0:T(8,128)(2,1)S(1)}, u32[]{:S(2)}, u32[]{:S(2)}) async-start(bf16[16,128,64]{1,2,0:T(8,128)(2,1)} %bitcast.98), calls=%async_computation.4 | async-start | bytes 524288 | tf_op jit(solution)/shard_map/all_to_all | solution.py:30
  231.2 2.9 copy-start.16
  231.5 12.9 %copy-start.10 = (f32[128,1,256]{2,1,0:T(1,128)S(1)}, f32[128,1,256]{2,1,0:T(1,128)}, u32[]{:S(2)}) copy-start(f32[128,1,256]{2,1,0:T(1,128)} %copy-done.9) | copy-start | bytes 393220
  241.0 54.6 %all-to-all-start.5 = ((bf16[8,128,64]{1,2,0:T(8,128)(2,1)}), bf16[8,128,64]{1,2,0:T(8,128)(2,1)S(1)}, u32[]{:S(2)}, u32[]{:S(2)}) async-start(bf16[8,128,64]{1,2,0:T(8,128)(2,1)} %broadcast_in_dim.44), calls=%async_computation.5 | async-start | bytes 262144 | tf_op jit(solution)/shard_map/all_to_all | solution.py:36
Sparse Core Ops, SparseCore 0:
  9.7 98.7 all-gather.1
  163.7 106.9 reduce-scatter.3
